TPU v7x, 8 devices: a whole 2x2x1 slice. The times are simulated.
8 devices in a mesh: dp: 1 (over z), tp: 2 (over y), ep: 4 (over x, core).
Axes of the slice: x: 2, y: 2, z: 1, core: 2. Of those that a mesh axis runs over, the one named last changes fastest.
Arguments:
- tokens: bfloat16 [8192, 768], P(('dp', 'ep', 'tp'))
- expert_ids: int32 [8192, 1], P(('dp', 'ep', 'tp'))
- gate_vals: float32 [8192, 1], P(('dp', 'ep', 'tp'))
- w_up: bfloat16 [32, 768, 3072], P('ep', None, 'tp')
- w_down: bfloat16 [32, 3072, 768], P('ep', 'tp')
Outputs:
- output: bfloat16 [8192, 768], P(('dp', 'ep', 'tp'))
All inputs are finite; a program needn't handle non-finite values.
Results may differ from a plain program's by a relative error of at most 0.001.
Values are sent between devices in bfloat16 or wider.
A program may use at most 1 GiB of HBM per device.

v0:
```python
import jax
import jax.numpy as jnp
from jax import lax
from jax.sharding import PartitionSpec as P


def capacity(tok_count, n_top, n_exp):
    return ((5 * tok_count * n_top) // (4 * n_exp) + 7) // 8 * 8


def slot_table(route_ids, n_exp, slot_cap):
    expert_hit = (route_ids[:, :, None] == jnp.arange(n_exp, dtype=jnp.int32)).astype(jnp.int32)
    chosen = jnp.sum(expert_hit, axis=1)
    prior_count = jnp.cumsum(chosen, axis=0) - chosen
    token_rank = jnp.sum(expert_hit * prior_count[:, None, :], axis=2)
    return jnp.where(token_rank < slot_cap, route_ids * slot_cap + token_rank, -1)


def solution(mesh):
    n_ep = mesh.shape['ep']
    row_spec = P(('dp', 'ep', 'tp'), None)

    def local_moe(tokens, expert_ids, gate_vals, w_up, w_down):
        tok_count, hidden = tokens.shape
        n_top = expert_ids.shape[1]
        local_exp = w_up.shape[0]
        n_exp = local_exp * n_ep
        slot_cap = capacity(tok_count, n_top, n_exp)
        n_slots = n_exp * slot_cap
        slot_ids = slot_table(expert_ids, n_exp, slot_cap)
        slot_iota = jnp.arange(n_slots, dtype=jnp.int32)
        pick_mat = jnp.zeros((n_slots, tok_count), jnp.bfloat16)
        for choice_idx in range(n_top):
            pick_mat = pick_mat + (slot_iota[:, None] == slot_ids[None, :, choice_idx]).astype(jnp.bfloat16)
        send_buf = jnp.dot(pick_mat, tokens, preferred_element_type=jnp.float32).astype(jnp.bfloat16)
        send_buf = send_buf.reshape(n_exp, slot_cap, hidden)
        arrived = lax.all_to_all(send_buf, 'ep', 0, 1, tiled=True)
        gathered = lax.all_gather(arrived, 'tp', axis=1, tiled=True)
        pre_act = jnp.einsum('ech,ehf->ecf', gathered, w_up, preferred_element_type=jnp.float32)
        hidden_act = jax.nn.gelu(pre_act, approximate=True).astype(jnp.bfloat16)
        part_out = jnp.einsum('ecf,efh->ech', hidden_act, w_down, preferred_element_type=jnp.float32)
        reduced = lax.psum_scatter(part_out, 'tp', scatter_dimension=1, tiled=True).astype(jnp.bfloat16)
        returned = lax.all_to_all(reduced, 'ep', 1, 0, tiled=True).reshape(n_slots, hidden)
        gate_sum = jnp.zeros((tok_count, hidden), jnp.float32)
        for choice_idx in range(n_top):
            pick_row = (slot_ids[:, choice_idx, None] == slot_iota[None, :]).astype(jnp.bfloat16)
            picked = jnp.dot(pick_row, returned, preferred_element_type=jnp.float32)
            gate_sum = gate_sum + gate_vals[:, choice_idx, None] * picked
        return gate_sum.astype(jnp.bfloat16)

    return jax.shard_map(local_moe, mesh=mesh,
                         in_specs=(row_spec, row_spec, row_spec, P('ep', None, 'tp'), P('ep', 'tp', None)),
                         out_specs=row_spec, check_vma=False)
```

profile of v0, /device:TPU:1, one launch (start us, length us, event | category | flops | bytes accessed | tf_op | source)
XLA Modules:
  0.0 254.8 jit_solution(16941261311714334224)
XLA Ops:
  6.5 0.0 copy-start
  6.5 0.0 all-gather.2.cloned.1.call-start
  6.5 0.8 fusion.22
  7.4 9.0 %reduce-window.6 = s32[32,8,128]{2,1,0:T(8,128)S(1)} reduce-window(s32[32,8,128]{2,1,0:T(8,128)S(1)} %fusion.22, s32[]{:T(128)} %constant.7.clone.1), window={size=1x1x128 pad=0_0x0_0x127_0}, to_apply=%region_0.0 | reduce-window | flops 4161536 | bytes 262148 | tf_op jit(solution)/shard_map/reduce-window
  16.4 0.1 slice.8
  16.5 0.1 copy.15
  16.6 0.1 copy.16
  16.7 0.1 broadcast_add_fusion
  16.8 0.7 fusion.21
  17.6 0.7 compare_select_fusion
  18.3 0.0 copy-done
  18.3 2.4 fusion.16
  20.7 27.3 %all_to_all.33 = bf16[32,40,768]{2,1,0:T(8,128)(2,1)S(1)} all-to-all(bf16[32,40,768]{2,1,0:T(8,128)(2,1)S(1)} %bitcast.41), channel_id=1, replica_groups=mesh['dp'=1,'tp'=2,'ep'=4] {'ep'}, dimensions={0} | all-to-all | bytes 3932160 | tf_op jit(solution)/shard_map/all_to_all | solution.py:37
  48.0 1.4 copy.17
  49.4 0.0 all-gather.2.cloned.1.call-update
  49.4 0.0 reduce-scatter.2.cloned.1.call-start
  49.5 51.4 %all-gather.2.cloned.1.call-done = bf16[8,320,768]{2,1,0:T(8,128)(2,1)} async-done(((bf16[8,160,768]{2,1,0:T(8,128)(2,1)}), bf16[8,320,768]{2,1,0:T(8,128)(2,1)}) %all-gather.2.cloned.1.call-update) | async-done | bytes 3932176 | tf_op jit(solution)/shard_map/all_gather | solution.py:38
  100.9 21.4 %fusion.8 = f32[8,320,768]{2,1,0:T(8,128)} fusion(bf16[8,1536,768]{2,1,0:T(8,128)(2,1)} %param.9, bf16[8,320,768]{2,1,0:T(8,128)(2,1)} %all-gather.2.cloned.1.call-done, bf16[8,768,1536]{2,1,0:T(8,128)(2,1)} %param.8), kind=kOutput, calls=%fused_computation.9 | convolution fusion | flops 12114984960 | bytes 49545216 | tf_op jit(solution)/shard_map/ecf,efh->ech/dot_general | solution.py:41
  122.4 0.0 reduce-scatter.2.cloned.1.call-update
  122.4 91.5 %reduce-scatter.2.cloned.1.call-done = f32[8,160,768]{2,1,0:T(8,128)} async-done(((f32[8,320,768]{2,1,0:T(8,128)}), f32[8,160,768]{2,1,0:T(8,128)}) %reduce-scatter.2.cloned.1.call-update) | async-done | bytes 3932176 | tf_op jit(solution)/shard_map/reduce_scatter | solution.py:42
  213.9 2.3 convert_element_type.28
  216.2 0.0 copy-start.2
  216.2 1.1 copy.18
  217.3 26.7 %all_to_all.34 = bf16[8,160,768]{2,0,1:T(8,128)(2,1)S(1)} all-to-all(bf16[8,160,768]{2,0,1:T(8,128)(2,1)S(1)} %copy.18), channel_id=1, replica_groups=mesh['dp'=1,'tp'=2,'ep'=4] {'ep'}, dimensions={1} | all-to-all | bytes 3932160 | tf_op jit(solution)/shard_map/all_to_all | solution.py:43
  244.0 0.4 copy.20
  244.3 0.0 copy-start.1
  244.4 0.0 copy-done.2
  244.4 3.6 %multiply_convert_fusion = bf16[1024,768]{1,0:T(8,128)(2,1)} fusion(bf16[1280,768]{1,0:T(8,128)(2,1)S(1)} %bitcast.40, s32[1024]{0:T(1024)S(1)} %bitcast.48, f32[1024]{0:T(1024)S(1)} %bitcast.49), kind=kOutput, calls=%fused_computation.19 | convolution fusion | flops 2016149504 | bytes 3547136 | tf_op jit(solution)/shard_map/dot_general | solution.py:47
  248.0 0.0 copy-done.1
  (2 shorter events, 0.0 us)
Async XLA Ops:
  6.5 11.7 %copy-start = (bf16[1024,768]{1,0:T(8,128)(2,1)S(1)}, bf16[1024,768]{1,0:T(8,128)(2,1)}, u32[]{:S(2)}) copy-start(bf16[1024,768]{1,0:T(8,128)(2,1)} %param.5) | copy-start | bytes 4718596
  6.5 94.4 %all-gather.2.cloned.1.call-start = ((), (), s32[]{:S(2)}) async-start(), calls=%async_computation.3 | async-start | bytes 5898240 | tf_op jit(solution)/shard_map/all_gather | solution.py:38
  49.4 164.4 %reduce-scatter.2.cloned.1.call-start = ((), (), s32[]{:S(2)}) async-start(), calls=%async_computation.4 | async-start | bytes 11796480 | tf_op jit(solution)/shard_map/reduce_scatter | solution.py:42
  216.2 28.2 %copy-start.2 = (f32[1024,1]{0,1:T(1,128)S(1)}, f32[1024,1]{0,1:T(1,128)}, u32[]{:S(2)}) copy-start(f32[1024,1]{0,1:T(1,128)} %param.7) | copy-start | bytes 12292
  244.3 3.6 %copy-start.1 = (bf16[1024,768]{1,0:T(8,128)(2,1)S(1)}, bf16[1024,768]{1,0:T(8,128)(2,1)}, u32[]{:S(2)}) copy-start(bf16[1024,768]{1,0:T(8,128)(2,1)} %param.5) | copy-start | bytes 4718596
Sparse Core Ops, SparseCore 0:
  49.6 51.3 all-gather.1
  122.5 91.2 reduce-scatter.1
where the time goes:
time: 256 us; the launch traced here: 255 us
  waiting for transfers between devices  143 us (56%)
  blocking collectives  54 us (21%)
  matrix products  27.5 us (11%)
  other arithmetic  13.7 us (5%)
  between operations  13.5 us (5%)
  local copies, waits for them, and re-layouts  3.19 us (1%)
    reduce_scatter x1, waiting for transfers between devices, local_moe(): lax.psum_scatter(part_out, 'tp', scatter_dimension=1, tiled=True)  91.5 us
    all_gather x1, waiting for transfers between devices, local_moe(): gathered = lax.all_gather(arrived, 'tp', axis=1, tiled=True)  51.4 us
    all_to_all x1, blocking collectives, local_moe(): arrived = lax.all_to_all(send_buf, 'ep', 0, 1, tiled=True)  27.3 us
    all_to_all x1, blocking collectives, local_moe(): lax.all_to_all(reduced, 'ep', 1, 0, tiled=True).reshape(n_slots, hidden)  26.7 us
    dot_general x1, matrix products, local_moe(): jnp.einsum('ecf,efh->ech', hidden_act, w_down, preferred_element_type=jnp...  21.4 us
    another operation x3, other arithmetic  9.15 us
  transfers between devices with their start and end apart: 2, of which 2 were waited for; matrix products, arithmetic and copies ran while one was open for 0% of the time, Pallas kernels for 0%

commit v1 on v0

v1 whole, which is shorter than its diff:
```python
import functools

import jax
import jax.numpy as jnp
from jax import lax
from jax.experimental import pallas as pl
from jax.experimental.pallas import tpu as pltpu
from jax.sharding import PartitionSpec as P

MESH = pl.DeviceIdType.MESH
W_SLOTS = 3


def capacity(tok_count, n_top, n_exp):
    return ((5 * tok_count * n_top) // (4 * n_exp) + 7) // 8 * 8


def moe_kernel(dims, tok_hbm, ids_ref, up_hbm, down_hbm, out_ref,
               tok_own, tok_peer, ids_peer, slot_own, slot_peer, slot_col,
               send_rows, rows, up_buf, down_buf, hid, mine, other, arrived, ret_send, ret_recv,
               tok_sem, w_sem, ids_ss, ids_rs, ytok_ss, ytok_rs, disp_ss, disp_rs,
               part_ss, part_rs, ret_ss, ret_rs, go_sem):
    n_tok, hidden, ffn, n_loc, cap, pad = dims
    n_exp = 4 * n_loc
    f32, bf16 = jnp.float32, jnp.bfloat16
    dp, tp, ep = lax.axis_index('dp'), lax.axis_index('tp'), lax.axis_index('ep')
    core = lax.rem(ep, 2)

    def rel_ep(d):
        flipped = lax.rem(ep + 2 * (d // 2), 4)
        return flipped + (d % 2) * (1 - 2 * lax.rem(flipped, 2))

    def dev(d):
        return (dp, tp, rel_ep(d))

    peer = (dp, 1 - tp, ep)
    partner = dev(1)

    def w_copies(n):
        slot, e = lax.rem(n, W_SLOTS), lax.rem(n, n_loc)
        return (pltpu.make_async_copy(up_hbm.at[e], up_buf.at[slot], w_sem.at[slot, 0]),
                pltpu.make_async_copy(down_hbm.at[e], down_buf.at[slot], w_sem.at[slot, 1]))

    def w_start(n):
        for cp in w_copies(n):
            cp.start()

    tok_cp = pltpu.make_async_copy(tok_hbm, tok_own, tok_sem)
    tok_cp.start()

    barrier = pltpu.get_barrier_semaphore()
    for target in (peer, dev(1), dev(2), dev(3)):
        pl.semaphore_signal(barrier, inc=1, device_id=target, device_id_type=MESH)
    pl.semaphore_wait(barrier, 4)

    ids_cp = pltpu.make_async_remote_copy(ids_ref, ids_peer, ids_ss, ids_rs, device_id=peer, device_id_type=MESH)
    ids_cp.start()
    tok_cp.wait()

    cut = n_tok * 7 // 8
    ytok = [pltpu.make_async_remote_copy(tok_own.at[pl.ds(a, n)], tok_peer.at[pl.ds(a, n)], ytok_ss.at[i],
                                         ytok_rs.at[i], device_id=peer, device_id_type=MESH)
            for i, (a, n) in enumerate(((0, cut), (cut, n_tok - cut)))]

    @pl.when(core == 0)
    def _():
        for cp in ytok:
            cp.start()

    for n in range(W_SLOTS):
        w_start(n)

    lane = 128
    tri = (lax.broadcasted_iota(jnp.int32, (lane, lane), 0)
           < lax.broadcasted_iota(jnp.int32, (lane, lane), 1)).astype(bf16)
    eye = (lax.broadcasted_iota(jnp.int32, (lane, lane), 0)
           == lax.broadcasted_iota(jnp.int32, (lane, lane), 1))
    exp_iota = lax.broadcasted_iota(jnp.int32, (n_exp, lane), 0)

    def route(ids, slots, column):
        counts = jnp.zeros((n_exp, 1), f32)
        for b in range(n_tok // lane):
            here = pl.ds(b * lane, lane)
            id_row = ids[:, here]
            hit = jnp.where(exp_iota == id_row, 1.0, 0.0).astype(f32)
            before = jnp.dot(hit.astype(bf16), tri, preferred_element_type=f32) + counts
            rank = jnp.sum(hit * before, axis=0, keepdims=True)
            counts = counts + jnp.sum(hit, axis=1, keepdims=True)
            slot = jnp.where(rank < cap, id_row.astype(f32) * cap + rank, -1.0)
            slots[:, here] = slot
            if column is not None:
                column[here, :] = jnp.sum(jnp.where(eye, slot, 0.0), axis=1, keepdims=True)

    route(ids_ref, slot_own, slot_col)
    ids_cp.wait_recv()
    route(ids_peer, slot_peer, None)

    @pl.when(core == 0)
    def _():
        ytok[0].wait_send()
        pl.semaphore_signal(go_sem, inc=1, device_id=partner, device_id_type=MESH)

    @pl.when(core == 1)
    def _():
        pl.semaphore_wait(go_sem, 1)
        for cp in ytok:
            cp.start()

    def disp_copy(e, d):
        return pltpu.make_async_remote_copy(
            send_rows.at[e, d - 1], rows.at[d % 2, e, pl.ds(2 * cap * (d // 2), 2 * cap)],
            disp_ss.at[e, d], disp_rs.at[e, d], device_id=dev(d), device_id_type=MESH)

    def dispatch():
        for cp in ytok:
            cp.wait_recv()

        def step(e, carry):
            k_iota = lax.broadcasted_iota(jnp.int32, (cap, 1), 0)
            target = jnp.concatenate([(k_iota + (rel_ep(d) * n_loc + e) * cap).astype(f32) for d in range(4)], axis=0)
            picked = []
            for slots, toks in ((slot_own, tok_own), (slot_peer, tok_peer)):
                pick = jnp.where(slots[...] == target, 1.0, 0.0).astype(bf16)
                picked.append(jnp.dot(pick, toks[...], preferred_element_type=f32))
            for d in range(4):
                part = slice(d * cap, (d + 1) * cap)
                block = jnp.concatenate([picked[0][part], picked[1][part]], axis=0).astype(bf16)
                if d == 0:
                    rows[0, e, pl.ds(0, 2 * cap)] = block
                else:
                    send_rows[e, d - 1] = block
            for d in (2, 3, 1):
                disp_copy(e, d).start()
            return carry

        lax.fori_loop(0, n_loc, step, 0)

    def part_copy(p, e, n):
        return pltpu.make_async_remote_copy(other.at[p, e], arrived.at[p, e], part_ss.at[n], part_rs.at[n],
                                            device_id=peer, device_id_type=MESH)

    def group_parity(g):
        return lax.rem(g + core, 2)

    def rows_wait(p, e, k):
        d = p + 2 * k
        pltpu.make_async_remote_copy(
            send_rows.at[0, 0], rows.at[p, e, pl.ds(2 * cap * k, 2 * cap)],
            disp_ss.at[e, d], disp_rs.at[e, d], device_id=peer, device_id_type=MESH).wait_recv()

    def experts(g):
        p = group_parity(g)

        def step(e, carry):
            n = g * n_loc + e
            slot = lax.rem(n, W_SLOTS)

            @pl.when(p == 1)
            def _():
                rows_wait(p, e, 0)
            rows_wait(p, e, 1)
            ups, downs = w_copies(n)
            ups.wait()
            x = rows[p, e]
            chunk = 512
            for j in range(ffn // chunk):
                cols = pl.ds(j * chunk, chunk)
                pre = jnp.dot(x, up_buf[slot, :, cols], preferred_element_type=f32)
                hid[:, cols] = jax.nn.gelu(pre, approximate=True).astype(bf16)
            downs.wait()
            part = jnp.dot(hid[...], down_buf[slot], preferred_element_type=f32)
            mine[p, e, pl.ds(0, cap)] = part[0:cap]
            other[p, e, pl.ds(0, cap)] = part[cap:2 * cap]
            mine[p, e, pl.ds(cap, cap)] = part[2 * cap:3 * cap]
            other[p, e, pl.ds(cap, cap)] = part[3 * cap:4 * cap]
            part_copy(p, e, n).start()

            @pl.when(n + W_SLOTS < 2 * n_loc)
            def _():
                w_start(n + W_SLOTS)
            return carry

        lax.fori_loop(0, n_loc, step, 0)

    @pl.when(core == 0)
    def _():
        dispatch()
    experts(0)

    @pl.when(core == 1)
    def _():
        dispatch()
    experts(1)

    def ret_copy(e, d):
        here = pl.ds(pl.multiple_of(d * pad, 16), pad)
        return pltpu.make_async_remote_copy(ret_send.at[e, d], ret_recv.at[e, here], ret_ss.at[e, d], ret_rs.at[e, d],
                                            device_id=dev(d), device_id_type=MESH)

    def reduce_step(g, e):
        p = group_parity(g)
        part_copy(p, e, g * n_loc + e).wait_recv()
        zeros = jnp.zeros((pad - cap, hidden), f32)
        blocks = []
        for k in range(2):
            here = pl.ds(k * cap, cap)
            total = mine[p, e, here] + arrived[p, e, here]
            blocks.append(jnp.concatenate([total, zeros], axis=0).astype(bf16))
        ret_send[e, p + 2] = blocks[1]
        ret_copy(e, p + 2).start()

        @pl.when(p == 0)
        def _():
            ret_recv[e, pl.ds(0, pad)] = blocks[0]

        @pl.when(p == 1)
        def _():
            ret_send[e, 1] = blocks[0]
            ret_copy(e, 1).start()

    out_rows = 256

    def combine(e, first):
        for d in (1, 2, 3):
            ret_copy(e, d).wait_recv()
        k_iota = lax.broadcasted_iota(jnp.int32, (1, 4 * pad), 1)
        block, rank = k_iota // pad, lax.rem(k_iota, pad)
        base = jnp.zeros((1, 4 * pad), jnp.int32)
        for d in range(4):
            base = base + jnp.where(block == d, (rel_ep(d) * n_loc + e) * cap, 0)
        target = jnp.where(rank < cap, base + rank, -2).astype(f32)

        def part(i, carry):
            here = pl.ds(pl.multiple_of(i * out_rows, out_rows), out_rows)
            pick = jnp.where(slot_col[here, :] == target, 1.0, 0.0).astype(bf16)
            got = jnp.dot(pick, ret_recv[e], preferred_element_type=f32)
            if first:
                out_ref[here, :] = got.astype(bf16)
            else:
                out_ref[here, :] = (out_ref[here, :].astype(f32) + got).astype(bf16)
            return carry

        lax.fori_loop(0, n_tok // out_rows, part, 0)

    def reduce_a(e, carry):
        reduce_step(0, e)
        return carry

    lax.fori_loop(0, n_loc, reduce_a, 0)

    @pl.when(core == 0)
    def _():
        combine(0, True)

        def rest(e, carry):
            combine(e, False)
            return carry

        lax.fori_loop(1, n_loc, rest, 0)

    reduce_step(1, 0)
    reduce_step(1, 1)

    @pl.when(core == 1)
    def _():
        combine(0, True)

    def reduce_b(e, carry):
        reduce_step(1, e)

        @pl.when(core == 1)
        def _():
            combine(e - 1, False)
        return carry

    lax.fori_loop(2, n_loc, reduce_b, 0)

    @pl.when(core == 1)
    def _():
        combine(n_loc - 1, False)

    ids_cp.wait_send()

    @pl.when(core == 1)
    def _():
        ytok[0].wait_send()
    ytok[1].wait_send()

    def drain(e, carry):
        for d in (1, 2, 3):
            disp_copy(e, d).wait_send()
            ret_copy(e, d).wait_send()
        for g in range(2):
            part_copy(g, e, g * n_loc + e).wait_send()
        return carry

    lax.fori_loop(0, n_loc, drain, 0)


def solution(mesh):
    n_ep, n_tp = mesh.shape['ep'], mesh.shape['tp']
    assert n_ep == 4 and n_tp == 2
    row_spec = P(('dp', 'ep', 'tp'), None)

    def local_moe(tokens, expert_ids, gate_vals, w_up, w_down):
        n_tok, hidden = tokens.shape
        n_loc, _, ffn = w_up.shape
        cap = capacity(n_tok, 1, n_loc * n_ep)
        pad = (cap + 15) // 16 * 16
        dims = (n_tok, hidden, ffn, n_loc, cap, pad)
        f32, bf16 = jnp.float32, jnp.bfloat16
        dma = pltpu.SemaphoreType.DMA
        vmem = pl.BlockSpec(memory_space=pltpu.VMEM)
        hbm = pl.BlockSpec(memory_space=pl.ANY)
        picked = pl.pallas_call(
            functools.partial(moe_kernel, dims),
            out_shape=jax.ShapeDtypeStruct((n_tok, hidden), bf16),
            in_specs=[hbm, vmem, hbm, hbm],
            out_specs=vmem,
            scratch_shapes=[
                pltpu.VMEM((n_tok, hidden), bf16),
                pltpu.VMEM((n_tok, hidden), bf16),
                pltpu.VMEM((1, n_tok), jnp.int32),
                pltpu.VMEM((1, n_tok), f32),
                pltpu.VMEM((1, n_tok), f32),
                pltpu.VMEM((n_tok, 1), f32),
                pltpu.VMEM((n_loc, 3, 2 * cap, hidden), bf16),
                pltpu.VMEM((2, n_loc, 4 * cap, hidden), bf16),
                pltpu.VMEM((W_SLOTS, hidden, ffn), bf16),
                pltpu.VMEM((W_SLOTS, ffn, hidden), bf16),
                pltpu.VMEM((4 * cap, ffn), bf16),
                pltpu.VMEM((2, n_loc, 2 * cap, hidden), f32),
                pltpu.VMEM((2, n_loc, 2 * cap, hidden), f32),
                pltpu.VMEM((2, n_loc, 2 * cap, hidden), f32),
                pltpu.VMEM((n_loc, 4, pad, hidden), bf16),
                pltpu.VMEM((n_loc, 4 * pad, hidden), bf16),
                dma, dma((W_SLOTS, 2)), dma, dma, dma((2,)), dma((2,)),
                dma((n_loc, 4)), dma((n_loc, 4)),
                dma((2 * n_loc,)), dma((2 * n_loc,)),
                dma((n_loc, 4)), dma((n_loc, 4)),
                pltpu.SemaphoreType.REGULAR,
            ],
            compiler_params=pltpu.CompilerParams(collective_id=0, has_side_effects=True, vmem_limit_bytes=62 << 20),
            name='moe_kernel',
        )(tokens, expert_ids.reshape(1, n_tok), w_up, w_down)
        return (gate_vals * picked.astype(f32)).astype(bf16)

    return jax.shard_map(local_moe, mesh=mesh,
                         in_specs=(row_spec, row_spec, row_spec, P('ep', None, 'tp'), P('ep', 'tp', None)),
                         out_specs=row_spec, check_vma=False)
```

time: 256 us -> 134 us (0.52)
  waiting for transfers between devices: 143 us -> 0 us
  Pallas kernels: 0 us -> 131 us
  blocking collectives: 54 us -> 0 us
  matrix products: 27.5 us -> 0 us
  between operations: 13.5 us -> 0.02 us
  other arithmetic: 13.7 us -> 2.87 us
  local copies, waits for them, and re-layouts: 3.19 us -> 0.01 us
    pallas_call x0 -> x1, Pallas kernels: none -> 131 us  [local_moe(): pl.pallas_call(functools.partial(moe_kernel, dims), out_shape=jax.ShapeDt...]
    reduce_scatter x1 -> x0, waiting for transfers between devices: 91.5 us -> none  [local_moe(): lax.psum_scatter(part_out, 'tp', scatter_dimension=1, tiled=True)]
    all_to_all x2 -> x0, blocking collectives: 54 us -> none  [the longest x1 27.3 us: local_moe(): arrived = lax.all_to_all(send_buf, 'ep', 0, 1, tiled=True)]
    all_gather x1 -> x0, waiting for transfers between devices: 51.4 us -> none  [local_moe(): gathered = lax.all_gather(arrived, 'tp', axis=1, tiled=True)]
    dot_general x3 -> x0, matrix products: 27.5 us -> none  [the longest x1 21.4 us: local_moe(): jnp.einsum('ecf,efh->ech', hidden_act, w_down, preferred_element_type=jnp...]
    another operation x3 -> x0, other arithmetic: 9.15 us -> none
  transfers between devices with their start and end apart: 2 -> 0, of which waited for: 2 -> 0; matrix products, arithmetic and copies ran while one was open for 0% -> 0% of each run, Pallas kernels for 0% -> 0%
where the time goes in v1:
time: 134 us
  Pallas kernels  131 us (98%)
  other arithmetic  2.87 us (2%)
    pallas_call x1, Pallas kernels, local_moe(): pl.pallas_call(functools.partial(moe_kernel, dims), out_shape=jax.ShapeDt...  131 us
    convert_element_type x1, other arithmetic, local_moe(): return (gate_vals * picked.astype(f32)).astype(bf16)  2.87 us

profile of v1, /device:TPU:1, one launch (start us, length us, event | category | flops | bytes accessed | tf_op | source)
XLA Modules:
  0.0 133.9 jit_solution(15068519325350938761)
XLA Ops:
  0.0 0.0 copy-start
  0.0 131.0 %moe_kernel.1 = bf16[1024,768]{1,0:T(8,128)(2,1)} custom-call(bf16[1024,768]{1,0:T(8,128)(2,1)} %tok_hbm.1, s32[1,1024]{1,0:T(1,128)} %bitcast.3, bf16[8,768,1536]{2,1,0:T(8,128)(2,1)} %up_hbm.1, bf16[8,1536,768]{2,1,0:T(8,128)(2,1)} %down_hbm.1), custom_call_target="tpu_custom_call" | custom-call | tf_op jit(solution)/shard_map/moe_kernel/pallas_call | solution.py:315
  131.0 0.0 copy-done
  131.0 2.9 %multiply_convert_fusion = bf16[1024,768]{1,0:T(8,128)(2,1)} fusion(bf16[1024,768]{1,0:T(8,128)(2,1)} %moe_kernel.1, f32[1024]{0:T(1024)S(1)} %bitcast.2), kind=kLoop, calls=%fused_computation | loop fusion | flops 2359296 | bytes 3149824 | tf_op jit(solution)/shard_map/convert_element_type | solution.py:346
Async XLA Ops:
  0.0 131.0 %copy-start = (f32[1024,1]{0,1:T(1,128)S(1)}, f32[1024,1]{0,1:T(1,128)}, u32[]{:S(2)}) copy-start(f32[1024,1]{0,1:T(1,128)} %param.7) | copy-start | bytes 12292

commit v2 on v0

v2 whole, which is shorter than its diff:
```python
import functools

import jax
import jax.numpy as jnp
from jax import lax
from jax.experimental import pallas as pl
from jax.experimental.pallas import tpu as pltpu
from jax.sharding import PartitionSpec as P

MESH = pl.DeviceIdType.MESH
W_SLOTS = 2
VMEM_MIB = 52


def capacity(tok_count, n_top, n_exp):
    return ((5 * tok_count * n_top) // (4 * n_exp) + 7) // 8 * 8


def moe_kernel(dims, tok_hbm, ids_ref, up_hbm, down_hbm, out_ref,
               tok_own, tok_peer, ids_peer, slot_own, slot_peer, idx_col, cnts,
               send_rows, rows, up_buf, down_buf, hid, part, terms,
               ysend, arrived, mine, ovf, ret_recv,
               tok_sem, w_sem, ids_ss, ids_rs, ytok_ss, ytok_rs, cnt_ss, cnt_rs, disp_ss, disp_rs,
               d2d_ss, d2d_rs, ovf_ss, ovf_rs, y_ss, y_rs, ret_ss, ret_rs, go_sem, part_free):
    n_tok, hidden, ffn, n_loc, cap, pad = dims
    n_exp = 4 * n_loc
    col_exp = 2 * n_loc
    col_slots = col_exp * cap
    region = n_tok // 2
    quarter = region // 2
    chunk = quarter // 2
    n_ovf = col_slots - region
    f32, bf16, i32 = jnp.float32, jnp.bfloat16, jnp.int32
    dp, tp, ep = lax.axis_index('dp'), lax.axis_index('tp'), lax.axis_index('ep')
    core = lax.rem(ep, 2)
    col = ep // 2
    iota = functools.partial(lax.broadcasted_iota, i32)

    def rel_ep(d):
        flipped = lax.rem(ep + 2 * (d // 2), 4)
        return flipped + (d % 2) * (1 - 2 * lax.rem(flipped, 2))

    def dev(d, h=0):
        return (dp, tp if h == 0 else 1 - tp, rel_ep(d))

    peer = dev(0, 1)
    partner = dev(1)
    others = [(h, d) for d in range(4) for h in range(2) if (h, d) != (0, 0)]

    def remote(src, dst, ss, rs, target):
        return pltpu.make_async_remote_copy(src, dst, ss, rs, device_id=target, device_id_type=MESH)

    def parity(g):
        return lax.rem(g + core, 2)

    def w_copies(n):
        slot, e = lax.rem(n, W_SLOTS), lax.rem(n, n_loc)
        return (pltpu.make_async_copy(up_hbm.at[e], up_buf.at[slot], w_sem.at[slot, 0]),
                pltpu.make_async_copy(down_hbm.at[e], down_buf.at[slot], w_sem.at[slot, 1]))

    def w_start(n):
        for cp in w_copies(n):
            cp.start()

    tok_cp = pltpu.make_async_copy(tok_hbm, tok_own, tok_sem)
    tok_cp.start()

    barrier = pltpu.get_barrier_semaphore()
    for h, d in others:
        pl.semaphore_signal(barrier, inc=1, device_id=dev(d, h), device_id_type=MESH)
    pl.semaphore_wait(barrier, len(others))

    ids_cp = remote(ids_ref, ids_peer, ids_ss, ids_rs, peer)
    ids_cp.start()
    tok_cp.wait()

    cut = n_tok * 31 // 32
    ytok = [remote(tok_own.at[pl.ds(a, n)], tok_peer.at[pl.ds(a, n)], ytok_ss.at[i], ytok_rs.at[i], peer)
            for i, (a, n) in enumerate(((0, cut), (cut, n_tok - cut)))]

    @pl.when(core == 0)
    def _():
        for cp in ytok:
            cp.start()

    for n in range(W_SLOTS):
        w_start(n)

    lane = 128
    tri = (iota((lane, lane), 0) < iota((lane, lane), 1)).astype(bf16)
    eye = iota((lane, lane), 0) == iota((lane, lane), 1)
    exp_iota = iota((n_exp, lane), 0)
    row_e, col_e = iota((n_exp, n_exp), 0), iota((n_exp, n_exp), 1)
    before_in_col = ((col_e < row_e) & (col_e // col_exp == row_e // col_exp)).astype(bf16)

    def hits(ids, b):
        id_row = ids[:, pl.ds(b * lane, lane)]
        return id_row, jnp.where(exp_iota == id_row, 1.0, 0.0).astype(f32)

    def route(ids, slots):
        counts = jnp.zeros((n_exp, 1), f32)
        for b in range(n_tok // lane):
            id_row, hit = hits(ids, b)
            before = jnp.dot(hit.astype(bf16), tri, preferred_element_type=f32) + counts
            rank = jnp.sum(hit * before, axis=0, keepdims=True)
            counts = counts + jnp.sum(hit, axis=1, keepdims=True)
            slots[:, pl.ds(b * lane, lane)] = jnp.where(rank < cap, id_row.astype(f32) * cap + rank, -1.0)
        return counts

    def cnt_copy(h, d):
        return remote(cnts.at[0, 0], cnts.at[h, d], cnt_ss.at[h, d], cnt_rs.at[h, d], dev(d, h))

    kept = jnp.minimum(route(ids_ref, slot_own), float(cap))
    kept = jnp.broadcast_to(kept, (n_exp, lane))
    cnts[0, 0] = kept

    def disp_copy(h, e, d):
        return remote(send_rows.at[h, e, d - 1, pl.ds(0, cap)], rows.at[d % 2, e, 2 * h + d // 2, pl.ds(0, cap)],
                      disp_ss.at[h, e, d], disp_rs.at[h, e, d], dev(d))

    def disp_start(h, e):
        for d in (2, 3, 1):
            disp_copy(h, e, d).start()

    def dispatch(h):
        slots, toks = (slot_own, tok_own) if h == 0 else (slot_peer, tok_peer)

        def step(e2, carry):
            k_iota = iota((cap, 1), 0)
            pair = [(2 * e2 + m, d) for m in range(2) for d in range(4)]
            target = jnp.concatenate([(k_iota + (rel_ep(d) * n_loc + e) * cap).astype(f32) for e, d in pair], axis=0)
            pick = jnp.where(slots[...] == target, 1.0, 0.0).astype(bf16)
            picked = jnp.dot(pick, toks[...], preferred_element_type=f32)
            for m, (e, d) in enumerate(pair):
                block = picked[m * cap:(m + 1) * cap].astype(bf16)
                if d == 0:
                    rows[0, e, 2 * h, pl.ds(0, cap)] = block
                else:
                    send_rows[h, e, d - 1, pl.ds(0, cap)] = block
            for m in range(2):
                if h == 1:
                    disp_start(h, 2 * e2 + m)
                else:
                    @pl.when((core == 0) | (e2 < n_loc // 4))
                    def _():
                        disp_start(h, 2 * e2 + m)
            return carry

        lax.fori_loop(0, n_loc // 2, step, 0)

    dispatch(0)

    for h, d in others:
        cnt_copy(h, d).start()

    first_row = jnp.dot(before_in_col, kept.astype(bf16), preferred_element_type=f32)
    for b in range(n_tok // lane):
        here = pl.ds(b * lane, lane)
        id_row, hit = hits(ids_ref, b)
        slot = slot_own[:, here]
        rank = slot - id_row.astype(f32) * cap
        joint = (jnp.sum(hit * first_row, axis=0, keepdims=True) + rank).astype(i32)
        home = id_row // col_exp
        stays = joint < region
        where_col = jnp.where(stays, home, 1 - home)
        q = jnp.where(stays, joint, 2 * region - 1 - joint)
        idx = lax.rem(q // chunk, 2) * region + (2 * where_col + q // quarter) * chunk + lax.rem(q, chunk)
        idx = jnp.where(slot < 0.0, -1.0, idx.astype(f32))
        idx_col[here, :] = jnp.sum(jnp.where(eye, idx, 0.0), axis=1, keepdims=True)

    ids_cp.wait_recv()
    route(ids_peer, slot_peer)

    @pl.when(core == 0)
    def _():
        ytok[0].wait_send()
        pl.semaphore_signal(go_sem, inc=1, device_id=partner, device_id_type=MESH)

    @pl.when(core == 1)
    def _():
        pl.semaphore_wait(go_sem, 1)
        for cp in ytok:
            cp.start()

    def d2d_copy(h, g, e):
        here = pl.ds(pl.multiple_of((core * n_loc + e) * cap, 8), cap)
        half = pl.ds(2 * h, 2)
        return remote(part.at[half, here], part.at[half, here], d2d_ss.at[h, g, e], d2d_rs.at[h, g, e], partner)

    def experts(g, extra):
        p = parity(g)

        def arrival(h, e, k):
            d = p + 2 * k
            remote(send_rows.at[0, 0, 0, pl.ds(0, cap)], rows.at[p, e, 2 * h + k, pl.ds(0, cap)],
                   disp_ss.at[h, e, d], disp_rs.at[h, e, d], peer).wait_recv()

        def step(e, carry):
            n = g * n_loc + e
            slot = lax.rem(n, W_SLOTS)
            for h in range(2):
                @pl.when(p == 1)
                def _():
                    arrival(h, e, 0)
                arrival(h, e, 1)
            ups, downs = w_copies(n)
            ups.wait()
            x = rows[p, e].reshape(4 * pad, hidden)
            width = 512
            for j in range(ffn // width):
                cols = pl.ds(j * width, width)
                pre = jnp.dot(x, up_buf[slot, :, cols], preferred_element_type=f32)
                hid[:, cols] = jax.nn.gelu(pre, approximate=True).astype(bf16)
            downs.wait()
            res = jnp.dot(hid[...], down_buf[slot], preferred_element_type=f32)
            here = pl.ds(pl.multiple_of((core * n_loc + e) * cap, 8), cap)
            for hk in range(4):
                part[hk, here] = res[hk * pad:hk * pad + cap]
            d2d_copy(1, g, e).start()
            d2d_copy(0, g, e).start()

            @pl.when(n + W_SLOTS < 2 * n_loc)
            def _():
                w_start(n + W_SLOTS)
            extra(e)
            return carry

        lax.fori_loop(0, n_loc, step, 0)

    slot_iota = iota((1, col_slots), 1)
    slot_exp, slot_rank = slot_iota // cap, lax.rem(slot_iota, cap)
    exp_match = iota((col_exp, col_slots), 0) == slot_exp
    before_exp = (iota((col_exp, col_exp), 1) < iota((col_exp, col_exp), 0)).astype(bf16)

    def positions(h, p, k):
        cnt = cnts[h, p + 2 * k, pl.ds(pl.multiple_of(col * col_exp, 8), col_exp), :]
        start = jnp.dot(before_exp, cnt.astype(bf16), preferred_element_type=f32)
        start_row = jnp.sum(jnp.where(exp_match, start[:, 0:1], 0.0), axis=0, keepdims=True)
        cnt_row = jnp.sum(jnp.where(exp_match, cnt[:, 0:1], 0.0), axis=0, keepdims=True)
        rank = slot_rank.astype(f32)
        return jnp.where(rank < cnt_row, start_row + rank, -1.0)

    def ovf_copy(h, g, k):
        p = parity(g)
        return remote(ovf.at[h, p, k], ovf.at[h, 1 - p, 1 - k], ovf_ss.at[h, g, k], ovf_rs.at[h, g, 1 - k], dev(3))

    def y_copy(p, k, i):
        here = pl.ds(i * chunk, chunk)
        return remote(ysend.at[p, k, here], arrived.at[p, k, here], y_ss.at[p, k, i], y_rs.at[p, k, i], peer)

    def compact(h, g):
        p = parity(g)
        dest = ysend if h == 1 else mine

        for k in (1, 0):
            where = positions(h, p, k)
            x = part[2 * h + k]
            hi = x.astype(bf16)
            rest = x - hi.astype(f32)
            mid = rest.astype(bf16)
            terms[pl.ds(0, col_slots)] = hi
            terms[pl.ds(col_slots, col_slots)] = mid
            terms[pl.ds(2 * col_slots, col_slots)] = (rest - mid.astype(f32)).astype(bf16)

            def take(target):
                pick = jnp.where(where == target.astype(f32), 1.0, 0.0).astype(bf16)
                return jnp.dot(jnp.concatenate([pick] * 3, axis=1), terms[...], preferred_element_type=f32)

            row = iota((quarter, 1), 0) + core * quarter

            @pl.when(core == 0)
            def _():
                got = take(jnp.concatenate([row, (col_slots - 1) - iota((n_ovf, 1), 0)], axis=0))
                dest[p, k] = got[0:quarter]
                ovf[h, p, k] = got[quarter:quarter + n_ovf]
                if h == 1:
                    y_copy(p, k, 0).start()
                    y_copy(p, k, 1).start()
                    ovf_copy(h, g, k).start()

            @pl.when(core == 1)
            def _():
                dest[p, k] = take(row)
                if h == 1:
                    y_copy(p, k, 0).start()

    def ovf_start(h, g):
        for k in (1, 0):
            ovf_copy(h, g, k).start()

    def d2d_wait(h, g):
        def wait(e, carry):
            d2d_copy(h, g, e).wait_recv()
            return carry

        lax.fori_loop(0, n_loc, wait, 0)

    def fill(h, g):
        p = parity(g)
        dest = ysend if h == 1 else mine

        @pl.when(core == 1)
        def _():
            for k in (1, 0):
                here = pl.ds(quarter - n_ovf, n_ovf)
                ovf_copy(h, g, 1 - k).wait_recv()
                dest[p, k, here] = dest[p, k, here] + ovf[h, p, k]
                if h == 1:
                    y_copy(p, k, 1).start()

    def ret_rows(p, k, i):
        start = (2 * p + k) * quarter + i * chunk
        return tok_peer.at[pl.ds(pl.multiple_of(start, chunk), chunk)]

    def ret_copy(p, k, i):
        d = p + 2 * k
        there = pl.ds(pl.multiple_of(i * region + ep * chunk, chunk), chunk)
        return remote(ret_rows(p, k, i), ret_recv.at[there], ret_ss.at[p, k, i], ret_rs.at[d, i], dev(d))

    def ret_wait(d, i):
        remote(tok_peer.at[pl.ds(0, chunk)], ret_recv.at[pl.ds(0, chunk)], ret_ss.at[0, 0, 0], ret_rs.at[d, i],
               peer).wait_recv()

    def reduce_chunk(g, k, i):
        p = parity(g)
        here = pl.ds(i * chunk, chunk)
        y_copy(p, k, i).wait_recv()
        total = (mine[p, k, here] + arrived[p, k, here]).astype(bf16)
        if k == 1:
            ret_rows(p, k, i)[...] = total
            ret_copy(p, k, i).start()
        else:
            @pl.when(p == 0)
            def _():
                ret_recv[pl.ds(pl.multiple_of(i * region + ep * chunk, chunk), chunk)] = total

            @pl.when(p == 1)
            def _():
                ret_rows(p, k, i)[...] = total
                ret_copy(p, k, i).start()

    out_rows = 256

    def combine(far, i, first=False):
        for d in ((2, 3) if far else (1,)):
            ret_wait(d, i)
        start = i * region + (lax.rem(col + far, 2)) * 2 * chunk
        here_r = pl.ds(pl.multiple_of(start, chunk), 2 * chunk)
        target = (iota((1, 2 * chunk), 1) + start).astype(f32)

        def some(j, carry):
            here = pl.ds(pl.multiple_of(j * out_rows, out_rows), out_rows)
            pick = jnp.where(idx_col[here, :] == target, 1.0, 0.0).astype(bf16)
            got = jnp.dot(pick, ret_recv[here_r, :], preferred_element_type=f32)
            if first:
                out_ref[here, :] = got.astype(bf16)
            else:
                out_ref[here, :] = (out_ref[here, :].astype(f32) + got).astype(bf16)
            return carry

        lax.fori_loop(0, n_tok // out_rows, some, 0)

    @pl.when(core == 0)
    def _():
        for cp in ytok:
            cp.wait_recv()
        dispatch(1)

    def during_b(e):
        @pl.when(e == n_loc // 2)
        def _():
            fill(1, 0)

            @pl.when(core == 0)
            def _():
                ovf_start(0, 0)

    experts(0, lambda e: None)

    @pl.when(core == 1)
    def _():
        for e in range(n_loc // 2, n_loc):
            disp_start(0, e)
    d2d_wait(1, 0)
    for h, d in others:
        cnt_copy(h, d).wait_recv()
    compact(1, 0)

    @pl.when(core == 1)
    def _():
        for cp in ytok:
            cp.wait_recv()
        dispatch(1)
    d2d_wait(0, 0)
    compact(0, 0)
    pl.semaphore_signal(part_free, inc=1, device_id=partner, device_id_type=MESH)
    pl.semaphore_wait(part_free, 1)

    def sent_a(e, carry):
        for h in range(2):
            d2d_copy(h, 0, e).wait_send()
        return carry

    lax.fori_loop(0, n_loc, sent_a, 0)
    experts(1, during_b)
    d2d_wait(1, 1)
    compact(1, 1)
    fill(0, 0)

    @pl.when(core == 0)
    def _():
        for k, i in ((1, 0), (1, 1), (0, 0), (0, 1)):
            reduce_chunk(0, k, i)

    @pl.when(core == 1)
    def _():
        for k, i in ((1, 0), (0, 0), (1, 1), (0, 1)):
            reduce_chunk(0, k, i)
    d2d_wait(0, 1)
    compact(0, 1)

    @pl.when(core == 0)
    def _():
        ovf_start(0, 1)
        reduce_chunk(1, 1, 0)
        reduce_chunk(1, 1, 1)
        combine(1, 0, True)
        combine(0, 0)
        combine(1, 1)
        combine(0, 1)
        reduce_chunk(1, 0, 0)
        reduce_chunk(1, 0, 1)

    @pl.when(core == 1)
    def _():
        fill(1, 1)
        reduce_chunk(1, 1, 0)
        reduce_chunk(1, 0, 0)
        fill(0, 1)
        combine(1, 0, True)
        reduce_chunk(1, 1, 1)
        combine(0, 0)
        combine(1, 1)
        reduce_chunk(1, 0, 1)
        combine(0, 1)

    ids_cp.wait_send()

    @pl.when(core == 1)
    def _():
        ytok[0].wait_send()
    ytok[1].wait_send()
    for h, d in others:
        cnt_copy(h, d).wait_send()

    def drain(e, carry):
        for h in range(2):
            for d in (1, 2, 3):
                disp_copy(h, e, d).wait_send()
            d2d_copy(h, 1, e).wait_send()
        return carry

    lax.fori_loop(0, n_loc, drain, 0)

    @pl.when(core == 0)
    def _():
        for h in range(2):
            for g in range(2):
                for k in range(2):
                    ovf_copy(h, g, k).wait_send()
    for i in range(2):
        for p in range(2):
            for k in range(2):
                y_copy(p, k, i).wait_send()
                if p + 2 * k > 0:
                    ret_copy(p, k, i).wait_send()


def solution(mesh):
    n_ep, n_tp = mesh.shape['ep'], mesh.shape['tp']
    assert n_ep == 4 and n_tp == 2
    row_spec = P(('dp', 'ep', 'tp'), None)

    def local_moe(tokens, expert_ids, gate_vals, w_up, w_down):
        n_tok, hidden = tokens.shape
        n_loc, _, ffn = w_up.shape
        cap = capacity(n_tok, 1, n_loc * n_ep)
        pad = (cap + 15) // 16 * 16
        dims = (n_tok, hidden, ffn, n_loc, cap, pad)
        quarter = n_tok // 4
        col_slots = 2 * n_loc * cap
        n_ovf = col_slots - 2 * quarter
        f32, bf16 = jnp.float32, jnp.bfloat16
        dma = pltpu.SemaphoreType.DMA
        vmem = pl.BlockSpec(memory_space=pltpu.VMEM)
        hbm = pl.BlockSpec(memory_space=pl.ANY)
        picked = pl.pallas_call(
            functools.partial(moe_kernel, dims),
            out_shape=jax.ShapeDtypeStruct((n_tok, hidden), bf16),
            in_specs=[hbm, vmem, hbm, hbm],
            out_specs=vmem,
            scratch_shapes=[
                pltpu.VMEM((n_tok, hidden), bf16),
                pltpu.VMEM((n_tok, hidden), bf16),
                pltpu.VMEM((1, n_tok), jnp.int32),
                pltpu.VMEM((1, n_tok), f32),
                pltpu.VMEM((1, n_tok), f32),
                pltpu.VMEM((n_tok, 1), f32),
                pltpu.VMEM((2, 4, 4 * n_loc, 128), f32),
                pltpu.VMEM((2, n_loc, 3, pad, hidden), bf16),
                pltpu.VMEM((2, n_loc, 4, pad, hidden), bf16),
                pltpu.VMEM((W_SLOTS, hidden, ffn), bf16),
                pltpu.VMEM((W_SLOTS, ffn, hidden), bf16),
                pltpu.VMEM((4 * pad, ffn), bf16),
                pltpu.VMEM((4, col_slots, hidden), f32),
                pltpu.VMEM((3 * col_slots, hidden), bf16),
                pltpu.VMEM((2, 2, quarter, hidden), f32),
                pltpu.VMEM((2, 2, quarter, hidden), f32),
                pltpu.VMEM((2, 2, quarter, hidden), f32),
                pltpu.VMEM((2, 2, 2, n_ovf, hidden), f32),
                pltpu.VMEM((n_tok, hidden), bf16),
                dma, dma((W_SLOTS, 2)), dma, dma, dma((2,)), dma((2,)), dma((2, 4)), dma((2, 4)),
                dma((2, n_loc, 4)), dma((2, n_loc, 4)),
                dma((2, 2, n_loc)), dma((2, 2, n_loc)),
                dma((2, 2, 2)), dma((2, 2, 2)),
                dma((2, 2, 2)), dma((2, 2, 2)),
                dma((2, 2, 2)), dma((4, 2)),
                pltpu.SemaphoreType.REGULAR,
                pltpu.SemaphoreType.REGULAR,
            ],
            compiler_params=pltpu.CompilerParams(collective_id=0, has_side_effects=True, vmem_limit_bytes=VMEM_MIB << 20),
            name='moe_kernel',
        )(tokens, expert_ids.reshape(1, n_tok), w_up, w_down)
        return (gate_vals * picked.astype(f32)).astype(bf16)

    return jax.shard_map(local_moe, mesh=mesh,
                         in_specs=(row_spec, row_spec, row_spec, P('ep', None, 'tp'), P('ep', 'tp', None)),
                         out_specs=row_spec, check_vma=False)
```

time: 256 us -> 119 us (0.46)
  waiting for transfers between devices: 143 us -> 0 us
  Pallas kernels: 0 us -> 117 us
  blocking collectives: 54 us -> 0 us
  matrix products: 27.5 us -> 0 us
  between operations: 13.5 us -> 0.02 us
  other arithmetic: 13.7 us -> 1.47 us
    pallas_call x0 -> x1, Pallas kernels: none -> 117 us  [local_moe(): pl.pallas_call(functools.partial(moe_kernel, dims), out_shape=jax.ShapeDt...]
    reduce_scatter x1 -> x0, waiting for transfers between devices: 91.5 us -> none  [local_moe(): lax.psum_scatter(part_out, 'tp', scatter_dimension=1, tiled=True)]
    all_to_all x2 -> x0, blocking collectives: 54 us -> none  [the longest x1 27.3 us: local_moe(): arrived = lax.all_to_all(send_buf, 'ep', 0, 1, tiled=True)]
    all_gather x1 -> x0, waiting for transfers between devices: 51.4 us -> none  [local_moe(): gathered = lax.all_gather(arrived, 'tp', axis=1, tiled=True)]
    dot_general x3 -> x0, matrix products: 27.5 us -> none  [the longest x1 21.4 us: local_moe(): jnp.einsum('ecf,efh->ech', hidden_act, w_down, preferred_element_type=jnp...]
    another operation x3 -> x0, other arithmetic: 9.15 us -> none
  transfers between devices with their start and end apart: 2 -> 0, of which waited for: 2 -> 0; matrix products, arithmetic and copies ran while one was open for 0% -> 0% of each run, Pallas kernels for 0% -> 0%
where the time goes in v2:
time: 119 us
  Pallas kernels  117 us (98%)
  other arithmetic  1.47 us (1%)
    pallas_call x1, Pallas kernels, local_moe(): pl.pallas_call(functools.partial(moe_kernel, dims), out_shape=jax.ShapeDt...  117 us

profile of v2, /device:TPU:1, one launch (start us, length us, event | category | flops | bytes accessed | tf_op | source)
XLA Modules:
  0.0 119.3 jit_solution(11039522151383703162)
XLA Ops:
  0.0 0.0 copy-start
  0.0 0.7 copy-done
  0.7 0.0 copy-start.1
  0.7 117.1 %moe_kernel.1 = bf16[1024,768]{1,0:T(8,128)(2,1)S(1)} custom-call(bf16[1024,768]{1,0:T(8,128)(2,1)} %tok_hbm.1, s32[1,1024]{1,0:T(1,128)S(1)} %bitcast.2, bf16[8,768,1536]{2,1,0:T(8,128)(2,1)} %up_hbm.1, bf16[8,1536,768]{2,1,0:T(8,128)(2,1)} %down_hbm.1), custom_call_target="tpu_custom_call" | custom-call | tf_op jit(solution)/shard_map/moe_kernel/pallas_call | solution.py:497
  117.8 0.0 copy-done.1
  117.8 1.5 %multiply_convert_fusion = bf16[1024,768]{1,0:T(8,128)(2,1)} fusion(bf16[1024,768]{1,0:T(8,128)(2,1)S(1)} %moe_kernel.1, f32[1024]{0:T(1024)S(1)} %bitcast.3), kind=kLoop, calls=%fused_computation | loop fusion | flops 2359296 | bytes 3149824 | tf_op jit(solution)/shard_map/convert_element_type | solution.py:534
Async XLA Ops:
  0.0 0.7 copy-start
  0.7 117.1 %copy-start.1 = (f32[1024,1]{0,1:T(1,128)S(1)}, f32[1024,1]{0,1:T(1,128)}, u32[]{:S(2)}) copy-start(f32[1024,1]{0,1:T(1,128)} %param.7) | copy-start | bytes 12292

commit v3 on v2

--- a/solution.py
+++ b/solution.py
@@ -16,11 +16,11 @@
     return ((5 * tok_count * n_top) // (4 * n_exp) + 7) // 8 * 8
 
 
-def moe_kernel(dims, tok_hbm, ids_ref, up_hbm, down_hbm, out_ref,
-               tok_own, tok_peer, ids_peer, slot_own, slot_peer, idx_col, cnts,
+def moe_kernel(dims, tok_hbm, ids_hbm, up_hbm, down_hbm, out_ref,
+               tok_own, tok_peer, ids_ref, ids_peer, slot_own, slot_peer, idx_col, cnts,
                send_rows, rows, up_buf, down_buf, hid, part, terms,
                ysend, arrived, mine, ovf, ret_recv,
-               tok_sem, w_sem, ids_ss, ids_rs, ytok_ss, ytok_rs, cnt_ss, cnt_rs, disp_ss, disp_rs,
+               tok_sem, ids_sem, w_sem, ids_ss, ids_rs, ytok_ss, ytok_rs, cnt_ss, cnt_rs, disp_ss, disp_rs,
                d2d_ss, d2d_rs, ovf_ss, ovf_rs, y_ss, y_rs, ret_ss, ret_rs, go_sem, part_free):
     n_tok, hidden, ffn, n_loc, cap, pad = dims
     n_exp = 4 * n_loc
@@ -55,21 +55,33 @@
 
     def w_copies(n):
         slot, e = lax.rem(n, W_SLOTS), lax.rem(n, n_loc)
-        return (pltpu.make_async_copy(up_hbm.at[e], up_buf.at[slot], w_sem.at[slot, 0]),
-                pltpu.make_async_copy(down_hbm.at[e], down_buf.at[slot], w_sem.at[slot, 1]))
+        halves = []
+        for i, (src, dst) in enumerate(((up_hbm, up_buf), (down_hbm, down_buf))):
+            size = src.shape[1] // 2
+            halves.append([pltpu.make_async_copy(src.at[e, pl.ds(m * size, size)], dst.at[slot, pl.ds(m * size, size)],
+                                                 w_sem.at[slot, i, m]) for m in range(2)])
+        return halves
+
+    def for_all(what, copies):
+        for cp in copies:
+            getattr(cp, what)()
 
     def w_start(n):
-        for cp in w_copies(n):
-            cp.start()
+        for half in w_copies(n):
+            for cp in half:
+                cp.start()
 
     tok_cp = pltpu.make_async_copy(tok_hbm, tok_own, tok_sem)
     tok_cp.start()
+    ids_load = pltpu.make_async_copy(ids_hbm, ids_ref, ids_sem)
+    ids_load.start()
 
     barrier = pltpu.get_barrier_semaphore()
     for h, d in others:
         pl.semaphore_signal(barrier, inc=1, device_id=dev(d, h), device_id_type=MESH)
     pl.semaphore_wait(barrier, len(others))
 
+    ids_load.wait()
     ids_cp = remote(ids_ref, ids_peer, ids_ss, ids_rs, peer)
     ids_cp.start()
     tok_cp.wait()
@@ -108,15 +120,15 @@
         return counts
 
     def cnt_copy(h, d):
-        return remote(cnts.at[0, 0], cnts.at[h, d], cnt_ss.at[h, d], cnt_rs.at[h, d], dev(d, h))
+        return remote(cnts.at[0], cnts.at[4 * h + d], cnt_ss, cnt_rs, dev(d, h))
 
     kept = jnp.minimum(route(ids_ref, slot_own), float(cap))
     kept = jnp.broadcast_to(kept, (n_exp, lane))
-    cnts[0, 0] = kept
+    cnts[0] = kept
 
     def disp_copy(h, e, d):
         return remote(send_rows.at[h, e, d - 1, pl.ds(0, cap)], rows.at[d % 2, e, 2 * h + d // 2, pl.ds(0, cap)],
-                      disp_ss.at[h, e, d], disp_rs.at[h, e, d], dev(d))
+                      disp_ss.at[h], disp_rs.at[d % 2, e], dev(d))
 
     def disp_start(h, e):
         for d in (2, 3, 1):
@@ -185,33 +197,39 @@
     def d2d_copy(h, g, e):
         here = pl.ds(pl.multiple_of((core * n_loc + e) * cap, 8), cap)
         half = pl.ds(2 * h, 2)
-        return remote(part.at[half, here], part.at[half, here], d2d_ss.at[h, g, e], d2d_rs.at[h, g, e], partner)
+        return remote(part.at[half, here], part.at[half, here], d2d_ss.at[h, g], d2d_rs.at[h, g], partner)
 
     def experts(g, extra):
         p = parity(g)
 
-        def arrival(h, e, k):
-            d = p + 2 * k
-            remote(send_rows.at[0, 0, 0, pl.ds(0, cap)], rows.at[p, e, 2 * h + k, pl.ds(0, cap)],
-                   disp_ss.at[h, e, d], disp_rs.at[h, e, d], peer).wait_recv()
+        def arrival(e, blocks):
+            here = rows.at[p, e, pl.ds(0, blocks), pl.ds(0, cap)]
+            remote(here, here, disp_ss.at[0], disp_rs.at[p, e], peer).wait_recv()
 
         def step(e, carry):
             n = g * n_loc + e
             slot = lax.rem(n, W_SLOTS)
-            for h in range(2):
-                @pl.when(p == 1)
-                def _():
-                    arrival(h, e, 0)
-                arrival(h, e, 1)
+
+            @pl.when(p == 1)
+            def _():
+                arrival(e, 4)
+
+            @pl.when(p == 0)
+            def _():
+                arrival(e, 2)
             ups, downs = w_copies(n)
-            ups.wait()
+            for_all('wait', ups)
             x = rows[p, e].reshape(4 * pad, hidden)
             width = 512
             for j in range(ffn // width):
                 cols = pl.ds(j * width, width)
                 pre = jnp.dot(x, up_buf[slot, :, cols], preferred_element_type=f32)
                 hid[:, cols] = jax.nn.gelu(pre, approximate=True).astype(bf16)
-            downs.wait()
+
+            @pl.when(n + W_SLOTS < 2 * n_loc)
+            def _():
+                for_all('start', w_copies(n + W_SLOTS)[0])
+            for_all('wait', downs)
             res = jnp.dot(hid[...], down_buf[slot], preferred_element_type=f32)
             here = pl.ds(pl.multiple_of((core * n_loc + e) * cap, 8), cap)
             for hk in range(4):
@@ -221,7 +239,7 @@
 
             @pl.when(n + W_SLOTS < 2 * n_loc)
             def _():
-                w_start(n + W_SLOTS)
+                for_all('start', w_copies(n + W_SLOTS)[1])
             extra(e)
             return carry
 
@@ -233,7 +251,7 @@
     before_exp = (iota((col_exp, col_exp), 1) < iota((col_exp, col_exp), 0)).astype(bf16)
 
     def positions(h, p, k):
-        cnt = cnts[h, p + 2 * k, pl.ds(pl.multiple_of(col * col_exp, 8), col_exp), :]
+        cnt = cnts[4 * h + p + 2 * k, pl.ds(pl.multiple_of(col * col_exp, 8), col_exp), :]
         start = jnp.dot(before_exp, cnt.astype(bf16), preferred_element_type=f32)
         start_row = jnp.sum(jnp.where(exp_match, start[:, 0:1], 0.0), axis=0, keepdims=True)
         cnt_row = jnp.sum(jnp.where(exp_match, cnt[:, 0:1], 0.0), axis=0, keepdims=True)
@@ -242,11 +260,11 @@
 
     def ovf_copy(h, g, k):
         p = parity(g)
-        return remote(ovf.at[h, p, k], ovf.at[h, 1 - p, 1 - k], ovf_ss.at[h, g, k], ovf_rs.at[h, g, 1 - k], dev(3))
+        return remote(ovf.at[h, p, k], ovf.at[h, 1 - p, 1 - k], ovf_ss.at[h], ovf_rs.at[h, g, 1 - k], dev(3))
 
     def y_copy(p, k, i):
         here = pl.ds(i * chunk, chunk)
-        return remote(ysend.at[p, k, here], arrived.at[p, k, here], y_ss.at[p, k, i], y_rs.at[p, k, i], peer)
+        return remote(ysend.at[p, k, here], arrived.at[p, k, here], y_ss.at[p], y_rs.at[p, k, i], peer)
 
     def compact(h, g):
         p = parity(g)
@@ -281,19 +299,25 @@
             @pl.when(core == 1)
             def _():
                 dest[p, k] = take(row)
-                if h == 1:
+                if h == 1 and (g == 0 or k == 1):
                     y_copy(p, k, 0).start()
 
     def ovf_start(h, g):
         for k in (1, 0):
             ovf_copy(h, g, k).start()
 
+    half_col = n_loc * cap
+
+    def d2d_all(h, g):
+        here = part.at[pl.ds(2 * h, 2), pl.ds(0, half_col)]
+        return remote(here, here, d2d_ss.at[h, g], d2d_rs.at[h, g], partner)
+
     def d2d_wait(h, g):
-        def wait(e, carry):
-            d2d_copy(h, g, e).wait_recv()
-            return carry
-
-        lax.fori_loop(0, n_loc, wait, 0)
+        d2d_all(h, g).wait_recv()
+
+    def d2d_drain(g):
+        for h in range(2):
+            d2d_all(h, g).wait_send()
 
     def fill(h, g):
         p = parity(g)
@@ -306,6 +330,8 @@
                 ovf_copy(h, g, 1 - k).wait_recv()
                 dest[p, k, here] = dest[p, k, here] + ovf[h, p, k]
                 if h == 1:
+                    if g == 1 and k == 0:
+                        y_copy(p, k, 0).start()
                     y_copy(p, k, 1).start()
 
     def ret_rows(p, k, i):
@@ -315,10 +341,10 @@
     def ret_copy(p, k, i):
         d = p + 2 * k
         there = pl.ds(pl.multiple_of(i * region + ep * chunk, chunk), chunk)
-        return remote(ret_rows(p, k, i), ret_recv.at[there], ret_ss.at[p, k, i], ret_rs.at[d, i], dev(d))
+        return remote(ret_rows(p, k, i), ret_recv.at[there], ret_ss, ret_rs.at[d, i], dev(d))
 
     def ret_wait(d, i):
-        remote(tok_peer.at[pl.ds(0, chunk)], ret_recv.at[pl.ds(0, chunk)], ret_ss.at[0, 0, 0], ret_rs.at[d, i],
+        remote(tok_peer.at[pl.ds(0, chunk)], ret_recv.at[pl.ds(0, chunk)], ret_ss, ret_rs.at[d, i],
                peer).wait_recv()
 
     def reduce_chunk(g, k, i):
@@ -348,17 +374,14 @@
         here_r = pl.ds(pl.multiple_of(start, chunk), 2 * chunk)
         target = (iota((1, 2 * chunk), 1) + start).astype(f32)
 
-        def some(j, carry):
-            here = pl.ds(pl.multiple_of(j * out_rows, out_rows), out_rows)
+        for j in range(n_tok // out_rows):
+            here = pl.ds(j * out_rows, out_rows)
             pick = jnp.where(idx_col[here, :] == target, 1.0, 0.0).astype(bf16)
             got = jnp.dot(pick, ret_recv[here_r, :], preferred_element_type=f32)
             if first:
                 out_ref[here, :] = got.astype(bf16)
             else:
                 out_ref[here, :] = (out_ref[here, :].astype(f32) + got).astype(bf16)
-            return carry
-
-        lax.fori_loop(0, n_tok // out_rows, some, 0)
 
     @pl.when(core == 0)
     def _():
@@ -382,8 +405,8 @@
         for e in range(n_loc // 2, n_loc):
             disp_start(0, e)
     d2d_wait(1, 0)
-    for h, d in others:
-        cnt_copy(h, d).wait_recv()
+    cnt_all = remote(cnts.at[pl.ds(1, 7)], cnts.at[pl.ds(1, 7)], cnt_ss, cnt_rs, peer)
+    cnt_all.wait_recv()
     compact(1, 0)
 
     @pl.when(core == 1)
@@ -396,32 +419,42 @@
     pl.semaphore_signal(part_free, inc=1, device_id=partner, device_id_type=MESH)
     pl.semaphore_wait(part_free, 1)
 
-    def sent_a(e, carry):
-        for h in range(2):
-            d2d_copy(h, 0, e).wait_send()
-        return carry
-
-    lax.fori_loop(0, n_loc, sent_a, 0)
+    d2d_drain(0)
     experts(1, during_b)
     d2d_wait(1, 1)
     compact(1, 1)
-    fill(0, 0)
+    d2d_wait(0, 1)
+    compact(0, 1)
 
     @pl.when(core == 0)
     def _():
+        ovf_start(0, 1)
         for k, i in ((1, 0), (1, 1), (0, 0), (0, 1)):
             reduce_chunk(0, k, i)
 
     @pl.when(core == 1)
     def _():
-        for k, i in ((1, 0), (0, 0), (1, 1), (0, 1)):
+        fill(0, 0)
+        for k, i in ((1, 0), (0, 0), (1, 1)):
             reduce_chunk(0, k, i)
-    d2d_wait(0, 1)
-    compact(0, 1)
+        fill(1, 1)
+        reduce_chunk(0, 0, 1)
+
+    ids_cp.wait_send()
+
+    @pl.when(core == 1)
+    def _():
+        ytok[0].wait_send()
+    ytok[1].wait_send()
+    cnt_all.wait_send()
+
+    for h in range(2):
+        sent = send_rows.at[h, :, :, pl.ds(0, cap)]
+        remote(sent, sent, disp_ss.at[h], disp_rs.at[0, 0], peer).wait_send()
+    d2d_drain(1)
 
     @pl.when(core == 0)
     def _():
-        ovf_start(0, 1)
         reduce_chunk(1, 1, 0)
         reduce_chunk(1, 1, 1)
         combine(1, 0, True)
@@ -433,47 +466,24 @@
 
     @pl.when(core == 1)
     def _():
-        fill(1, 1)
         reduce_chunk(1, 1, 0)
-        reduce_chunk(1, 0, 0)
         fill(0, 1)
         combine(1, 0, True)
         reduce_chunk(1, 1, 1)
+        reduce_chunk(1, 0, 0)
         combine(0, 0)
         combine(1, 1)
         reduce_chunk(1, 0, 1)
         combine(0, 1)
 
-    ids_cp.wait_send()
-
-    @pl.when(core == 1)
-    def _():
-        ytok[0].wait_send()
-    ytok[1].wait_send()
-    for h, d in others:
-        cnt_copy(h, d).wait_send()
-
-    def drain(e, carry):
+    @pl.when(core == 0)
+    def _():
         for h in range(2):
-            for d in (1, 2, 3):
-                disp_copy(h, e, d).wait_send()
-            d2d_copy(h, 1, e).wait_send()
-        return carry
-
-    lax.fori_loop(0, n_loc, drain, 0)
-
-    @pl.when(core == 0)
-    def _():
-        for h in range(2):
-            for g in range(2):
-                for k in range(2):
-                    ovf_copy(h, g, k).wait_send()
-    for i in range(2):
-        for p in range(2):
-            for k in range(2):
-                y_copy(p, k, i).wait_send()
-                if p + 2 * k > 0:
-                    ret_copy(p, k, i).wait_send()
+            remote(ovf.at[h], ovf.at[h], ovf_ss.at[h], ovf_rs.at[0, 0, 0], peer).wait_send()
+    for p in range(2):
+        remote(ysend.at[p], ysend.at[p], y_ss.at[p], y_rs.at[0, 0, 0], peer).wait_send()
+    ret_rest = tok_peer.at[pl.ds(quarter, 3 * quarter)]
+    remote(ret_rest, ret_rest, ret_ss, ret_rs.at[0, 0], peer).wait_send()
 
 
 def solution(mesh):
@@ -497,16 +507,17 @@
         picked = pl.pallas_call(
             functools.partial(moe_kernel, dims),
             out_shape=jax.ShapeDtypeStruct((n_tok, hidden), bf16),
-            in_specs=[hbm, vmem, hbm, hbm],
+            in_specs=[hbm, hbm, hbm, hbm],
             out_specs=vmem,
             scratch_shapes=[
                 pltpu.VMEM((n_tok, hidden), bf16),
                 pltpu.VMEM((n_tok, hidden), bf16),
                 pltpu.VMEM((1, n_tok), jnp.int32),
+                pltpu.VMEM((1, n_tok), jnp.int32),
                 pltpu.VMEM((1, n_tok), f32),
                 pltpu.VMEM((1, n_tok), f32),
                 pltpu.VMEM((n_tok, 1), f32),
-                pltpu.VMEM((2, 4, 4 * n_loc, 128), f32),
+                pltpu.VMEM((8, 4 * n_loc, 128), f32),
                 pltpu.VMEM((2, n_loc, 3, pad, hidden), bf16),
                 pltpu.VMEM((2, n_loc, 4, pad, hidden), bf16),
                 pltpu.VMEM((W_SLOTS, hidden, ffn), bf16),
@@ -519,18 +530,15 @@
                 pltpu.VMEM((2, 2, quarter, hidden), f32),
                 pltpu.VMEM((2, 2, 2, n_ovf, hidden), f32),
                 pltpu.VMEM((n_tok, hidden), bf16),
-                dma, dma((W_SLOTS, 2)), dma, dma, dma((2,)), dma((2,)), dma((2, 4)), dma((2, 4)),
-                dma((2, n_loc, 4)), dma((2, n_loc, 4)),
-                dma((2, 2, n_loc)), dma((2, 2, n_loc)),
-                dma((2, 2, 2)), dma((2, 2, 2)),
-                dma((2, 2, 2)), dma((2, 2, 2)),
-                dma((2, 2, 2)), dma((4, 2)),
+                dma, dma, dma((W_SLOTS, 2, 2)), dma, dma, dma((2,)), dma((2,)), dma, dma,
+                dma((2,)), dma((2, n_loc)), dma((2, 2)), dma((2, 2)), dma((2,)), dma((2, 2, 2)),
+                dma((2,)), dma((2, 2, 2)), dma, dma((4, 2)),
                 pltpu.SemaphoreType.REGULAR,
                 pltpu.SemaphoreType.REGULAR,
             ],
             compiler_params=pltpu.CompilerParams(collective_id=0, has_side_effects=True, vmem_limit_bytes=VMEM_MIB << 20),
             name='moe_kernel',
-        )(tokens, expert_ids.reshape(1, n_tok), w_up, w_down)
+        )(tokens, pltpu.with_memory_space_constraint(expert_ids.reshape(1, n_tok), pltpu.HBM), w_up, w_down)
         return (gate_vals * picked.astype(f32)).astype(bf16)
 
     return jax.shard_map(local_moe, mesh=mesh,

time: 119 us -> 115 us (0.966)
  Pallas kernels: 117 us -> 114 us
    pallas_call x1, Pallas kernels: 117 us -> 114 us  [local_moe(): pl.pallas_call(functools.partial(moe_kernel, dims), out_shape=jax.ShapeDt...]
where the time goes in v3:
time: 115 us
  Pallas kernels  114 us (99%)
  other arithmetic  1.47 us (1%)
    pallas_call x1, Pallas kernels, local_moe(): pl.pallas_call(functools.partial(moe_kernel, dims), out_shape=jax.ShapeDt...  114 us

profile of v3, /device:TPU:1, one launch (start us, length us, event | category | flops | bytes accessed | tf_op | source)
XLA Modules:
  0.0 115.2 jit_solution(4244636999814041052)
XLA Ops:
  0.0 0.0 copy-start
  0.0 113.7 %moe_kernel.1 = bf16[1024,768]{1,0:T(8,128)(2,1)S(1)} custom-call(bf16[1024,768]{1,0:T(8,128)(2,1)} %tok_hbm.1, s32[1,1024]{1,0:T(1,128)} %bitcast.3, bf16[8,768,1536]{2,1,0:T(8,128)(2,1)} %up_hbm.1, bf16[8,1536,768]{2,1,0:T(8,128)(2,1)} %down_hbm.1), custom_call_target="tpu_custom_call" | custom-call | tf_op jit(solution)/shard_map/moe_kernel/pallas_call | solution.py:507
  113.7 0.0 copy-done
  113.7 1.5 %multiply_convert_fusion = bf16[1024,768]{1,0:T(8,128)(2,1)} fusion(bf16[1024,768]{1,0:T(8,128)(2,1)S(1)} %moe_kernel.1, f32[1024]{0:T(1024)S(1)} %bitcast.2), kind=kLoop, calls=%fused_computation | loop fusion | flops 2359296 | bytes 3149824 | tf_op jit(solution)/shard_map/convert_element_type | solution.py:542
Async XLA Ops:
  0.0 113.7 %copy-start = (f32[1024,1]{0,1:T(1,128)S(1)}, f32[1024,1]{0,1:T(1,128)}, u32[]{:S(2)}) copy-start(f32[1024,1]{0,1:T(1,128)} %param.7) | copy-start | bytes 12292

commit v4 on v3

--- a/solution.py
+++ b/solution.py
@@ -86,9 +86,10 @@
     ids_cp.start()
     tok_cp.wait()
 
+    half_tok = n_tok // 2
     cut = n_tok * 31 // 32
     ytok = [remote(tok_own.at[pl.ds(a, n)], tok_peer.at[pl.ds(a, n)], ytok_ss.at[i], ytok_rs.at[i], peer)
-            for i, (a, n) in enumerate(((0, cut), (cut, n_tok - cut)))]
+            for i, (a, n) in enumerate(((0, half_tok), (half_tok, cut - half_tok), (cut, n_tok - cut)))]
 
     @pl.when(core == 0)
     def _():
@@ -134,15 +135,21 @@
         for d in (2, 3, 1):
             disp_copy(h, e, d).start()
 
-    def dispatch(h):
+    def dispatch(h, stage=0):
         slots, toks = (slot_own, tok_own) if h == 0 else (slot_peer, tok_peer)
 
         def step(e2, carry):
             k_iota = iota((cap, 1), 0)
             pair = [(2 * e2 + m, d) for m in range(2) for d in range(4)]
             target = jnp.concatenate([(k_iota + (rel_ep(d) * n_loc + e) * cap).astype(f32) for e, d in pair], axis=0)
-            pick = jnp.where(slots[...] == target, 1.0, 0.0).astype(bf16)
-            picked = jnp.dot(pick, toks[...], preferred_element_type=f32)
+            span = [pl.ds(0, n_tok), pl.ds(0, half_tok), pl.ds(half_tok, half_tok)][stage]
+            pick = jnp.where(slots[:, span] == target, 1.0, 0.0).astype(bf16)
+            picked = jnp.dot(pick, toks[span, :], preferred_element_type=f32)
+            if stage == 1:
+                part[e2, pl.ds(0, 8 * cap)] = picked
+                return carry
+            if stage == 2:
+                picked = picked + part[e2, pl.ds(0, 8 * cap)]
             for m, (e, d) in enumerate(pair):
                 block = picked[m * cap:(m + 1) * cap].astype(bf16)
                 if d == 0:
@@ -185,7 +192,10 @@
 
     @pl.when(core == 0)
     def _():
+        ytok[0].wait_recv()
+        dispatch(1, 1)
         ytok[0].wait_send()
+        ytok[1].wait_send()
         pl.semaphore_signal(go_sem, inc=1, device_id=partner, device_id_type=MESH)
 
     @pl.when(core == 1)
@@ -266,19 +276,26 @@
         here = pl.ds(i * chunk, chunk)
         return remote(ysend.at[p, k, here], arrived.at[p, k, here], y_ss.at[p], y_rs.at[p, k, i], peer)
 
+    def split(block, half):
+        start = pl.multiple_of(half * half_col, 64)
+        x = part[block, pl.ds(start, half_col)]
+        hi = x.astype(bf16)
+        rest = x - hi.astype(f32)
+        mid = rest.astype(bf16)
+        low = (rest - mid.astype(f32)).astype(bf16)
+        for t, term in enumerate((hi, mid, low)):
+            terms[pl.ds(pl.multiple_of(start + t * col_slots, 64), half_col)] = term
+
     def compact(h, g):
         p = parity(g)
         dest = ysend if h == 1 else mine
 
         for k in (1, 0):
             where = positions(h, p, k)
-            x = part[2 * h + k]
-            hi = x.astype(bf16)
-            rest = x - hi.astype(f32)
-            mid = rest.astype(bf16)
-            terms[pl.ds(0, col_slots)] = hi
-            terms[pl.ds(col_slots, col_slots)] = mid
-            terms[pl.ds(2 * col_slots, col_slots)] = (rest - mid.astype(f32)).astype(bf16)
+            split(2 * h + k, core)
+            if k == 1:
+                d2d_wait(h, g)
+            split(2 * h + k, 1 - core)
 
             def take(target):
                 pick = jnp.where(where == target.astype(f32), 1.0, 0.0).astype(bf16)
@@ -286,8 +303,20 @@
 
             row = iota((quarter, 1), 0) + core * quarter
 
+            early = h == 1 and g == 0 and k == 1
+            if early:
+                dest[p, k, pl.ds(0, chunk)] = take(row[0:chunk])
+                y_copy(p, k, 0).start()
+
             @pl.when(core == 0)
             def _():
+                if early:
+                    got = take(jnp.concatenate([row[chunk:], (col_slots - 1) - iota((n_ovf, 1), 0)], axis=0))
+                    dest[p, k, pl.ds(chunk, chunk)] = got[0:chunk]
+                    ovf[h, p, k] = got[chunk:chunk + n_ovf]
+                    y_copy(p, k, 1).start()
+                    ovf_copy(h, g, k).start()
+                    return
                 got = take(jnp.concatenate([row, (col_slots - 1) - iota((n_ovf, 1), 0)], axis=0))
                 dest[p, k] = got[0:quarter]
                 ovf[h, p, k] = got[quarter:quarter + n_ovf]
@@ -298,6 +327,9 @@
 
             @pl.when(core == 1)
             def _():
+                if early:
+                    dest[p, k, pl.ds(chunk, chunk)] = take(row[chunk:])
+                    return
                 dest[p, k] = take(row)
                 if h == 1 and (g == 0 or k == 1):
                     y_copy(p, k, 0).start()
@@ -385,9 +417,9 @@
 
     @pl.when(core == 0)
     def _():
-        for cp in ytok:
+        for cp in ytok[1:]:
             cp.wait_recv()
-        dispatch(1)
+        dispatch(1, 2)
 
     def during_b(e):
         @pl.when(e == n_loc // 2)
@@ -398,15 +430,14 @@
             def _():
                 ovf_start(0, 0)
 
+    cnt_all = remote(cnts.at[pl.ds(1, 7)], cnts.at[pl.ds(1, 7)], cnt_ss, cnt_rs, peer)
+    cnt_all.wait_recv()
     experts(0, lambda e: None)
 
     @pl.when(core == 1)
     def _():
         for e in range(n_loc // 2, n_loc):
             disp_start(0, e)
-    d2d_wait(1, 0)
-    cnt_all = remote(cnts.at[pl.ds(1, 7)], cnts.at[pl.ds(1, 7)], cnt_ss, cnt_rs, peer)
-    cnt_all.wait_recv()
     compact(1, 0)
 
     @pl.when(core == 1)
@@ -414,16 +445,13 @@
         for cp in ytok:
             cp.wait_recv()
         dispatch(1)
-    d2d_wait(0, 0)
     compact(0, 0)
     pl.semaphore_signal(part_free, inc=1, device_id=partner, device_id_type=MESH)
     pl.semaphore_wait(part_free, 1)
 
     d2d_drain(0)
     experts(1, during_b)
-    d2d_wait(1, 1)
     compact(1, 1)
-    d2d_wait(0, 1)
     compact(0, 1)
 
     @pl.when(core == 0)
@@ -445,7 +473,8 @@
     @pl.when(core == 1)
     def _():
         ytok[0].wait_send()
-    ytok[1].wait_send()
+        ytok[1].wait_send()
+    ytok[2].wait_send()
     cnt_all.wait_send()
 
     for h in range(2):
@@ -530,7 +559,7 @@
                 pltpu.VMEM((2, 2, quarter, hidden), f32),
                 pltpu.VMEM((2, 2, 2, n_ovf, hidden), f32),
                 pltpu.VMEM((n_tok, hidden), bf16),
-                dma, dma, dma((W_SLOTS, 2, 2)), dma, dma, dma((2,)), dma((2,)), dma, dma,
+                dma, dma, dma((W_SLOTS, 2, 2)), dma, dma, dma((3,)), dma((3,)), dma, dma,
                 dma((2,)), dma((2, n_loc)), dma((2, 2)), dma((2, 2)), dma((2,)), dma((2, 2, 2)),
                 dma((2,)), dma((2, 2, 2)), dma, dma((4, 2)),
                 pltpu.SemaphoreType.REGULAR,

time: 115 us -> 114 us (level)
  no operation moved by 1% of the time
where the time goes in v4:
time: 114 us
  Pallas kernels  113 us (99%)
  other arithmetic  1.47 us (1%)
    pallas_call x1, Pallas kernels, local_moe(): pl.pallas_call(functools.partial(moe_kernel, dims), out_shape=jax.ShapeDt...  113 us

profile of v4, /device:TPU:1, one launch (start us, length us, event | category | flops | bytes accessed | tf_op | source)
XLA Modules:
  0.0 114.1 jit_solution(14394618184997107780)
XLA Ops:
  0.0 0.0 copy-start
  0.0 112.6 %moe_kernel.1 = bf16[1024,768]{1,0:T(8,128)(2,1)S(1)} custom-call(bf16[1024,768]{1,0:T(8,128)(2,1)} %tok_hbm.1, s32[1,1024]{1,0:T(1,128)} %bitcast.3, bf16[8,768,1536]{2,1,0:T(8,128)(2,1)} %up_hbm.1, bf16[8,1536,768]{2,1,0:T(8,128)(2,1)} %down_hbm.1), custom_call_target="tpu_custom_call" | custom-call | tf_op jit(solution)/shard_map/moe_kernel/pallas_call | solution.py:536
  112.6 0.0 copy-done
  112.6 1.5 %multiply_convert_fusion = bf16[1024,768]{1,0:T(8,128)(2,1)} fusion(bf16[1024,768]{1,0:T(8,128)(2,1)S(1)} %moe_kernel.1, f32[1024]{0:T(1024)S(1)} %bitcast.2), kind=kLoop, calls=%fused_computation | loop fusion | flops 2359296 | bytes 3149824 | tf_op jit(solution)/shard_map/convert_element_type | solution.py:571
Async XLA Ops:
  0.0 112.6 %copy-start = (f32[1024,1]{0,1:T(1,128)S(1)}, f32[1024,1]{0,1:T(1,128)}, u32[]{:S(2)}) copy-start(f32[1024,1]{0,1:T(1,128)} %param.7) | copy-start | bytes 12292

commit v5 on v4

--- a/solution.py
+++ b/solution.py
@@ -194,8 +194,8 @@
     def _():
         ytok[0].wait_recv()
         dispatch(1, 1)
-        ytok[0].wait_send()
-        ytok[1].wait_send()
+        for cp in ytok:
+            cp.wait_send()
         pl.semaphore_signal(go_sem, inc=1, device_id=partner, device_id_type=MESH)
 
     @pl.when(core == 1)
@@ -472,9 +472,8 @@
 
     @pl.when(core == 1)
     def _():
-        ytok[0].wait_send()
-        ytok[1].wait_send()
-    ytok[2].wait_send()
+        for cp in ytok:
+            cp.wait_send()
     cnt_all.wait_send()
 
     for h in range(2):

time: 114 us -> 114 us (level)
  no operation moved by 1% of the time
where the time goes in v5:
time: 114 us
  Pallas kernels  113 us (99%)
  other arithmetic  1.47 us (1%)
    pallas_call x1, Pallas kernels, local_moe(): pl.pallas_call(functools.partial(moe_kernel, dims), out_shape=jax.ShapeDt...  113 us

profile of v5, /device:TPU:1, one launch (start us, length us, event | category | flops | bytes accessed | tf_op | source)
XLA Modules:
  0.0 114.1 jit_solution(1143138144859425437)
XLA Ops:
  0.0 0.0 copy-start
  0.0 112.6 %moe_kernel.1 = bf16[1024,768]{1,0:T(8,128)(2,1)S(1)} custom-call(bf16[1024,768]{1,0:T(8,128)(2,1)} %tok_hbm.1, s32[1,1024]{1,0:T(1,128)} %bitcast.3, bf16[8,768,1536]{2,1,0:T(8,128)(2,1)} %up_hbm.1, bf16[8,1536,768]{2,1,0:T(8,128)(2,1)} %down_hbm.1), custom_call_target="tpu_custom_call" | custom-call | tf_op jit(solution)/shard_map/moe_kernel/pallas_call | solution.py:535
  112.6 0.0 copy-done
  112.6 1.5 %multiply_convert_fusion = bf16[1024,768]{1,0:T(8,128)(2,1)} fusion(bf16[1024,768]{1,0:T(8,128)(2,1)S(1)} %moe_kernel.1, f32[1024]{0:T(1024)S(1)} %bitcast.2), kind=kLoop, calls=%fused_computation | loop fusion | flops 2359296 | bytes 3149824 | tf_op jit(solution)/shard_map/convert_element_type | solution.py:570
Async XLA Ops:
  0.0 112.6 %copy-start = (f32[1024,1]{0,1:T(1,128)S(1)}, f32[1024,1]{0,1:T(1,128)}, u32[]{:S(2)}) copy-start(f32[1024,1]{0,1:T(1,128)} %param.7) | copy-start | bytes 12292
